TPU v7x, 32 devices: a whole 2x2x4 slice. The times are simulated.
32 devices in a mesh: leaf: 4 (over x, core), blk: 8 (over z, y).
Axes of the slice: x: 2, y: 2, z: 4, core: 2. Of those that a mesh axis runs over, the one named last changes fastest.
Arguments:
- right_side: float32 [4, 4, 8, 384], P(None, 'leaf', 'blk'), may hold values from -6 to 6
- diag_inverse: bfloat16 [4, 8, 128, 7168], P('leaf', 'blk'), as said below
- update_factor: bfloat16 [4, 8, 128, 10240], P('leaf', 'blk'), may hold values from -0.09375 to 0.09375
- live_blocks: int32 [7], replicated, may hold values from 1 to 32, as said below
Outputs:
- forward_solution: float32 [4, 4, 8, 384], P(None, 'leaf', 'blk')
- solution: float32 [4, 4, 8, 384], P(None, 'leaf', 'blk')
Inputs may be any that keep to these rules, and one draw needn't show every extreme that they name: `live_blocks`: A supernode with 2^l * 8 block-rows (level l, listed level by level from level 0, by group within a level) has between a quarter of them (at least 1) and all of them live; the root supernode (the last entry) has all of them live. `diag_inverse`: each level's inverse diagonal block is lower triangular in its supernode's row order, with a positive diagonal.
All inputs are finite; a program needn't handle non-finite values.
Results may differ from a plain program's by a relative error of at most 0.009.
Values sent between devices are 32-bit elements; how exact they have to be, the bound alone decides.
No kernel may reach another device: no remote copies, remote signals or barrier semaphores. Data moves between devices by JAX's collectives and lax.ppermute only.
A program may use at most 128 MiB of HBM per device.

v0:
```python
import jax
import jax.numpy as jnp
from jax import lax
from jax.sharding import PartitionSpec as P


def swapped(block, axis, apart):
    count = lax.axis_size(axis)
    route = []
    for low in range(count):
        high = low | 1 << apart
        if high != low and high < count:
            route += [(low, high), (high, low)]
    return lax.ppermute(block, axis, route)


def group_sum(partial_value, height):
    current = lax.psum(partial_value, "blk")
    for bit_number in range(height):
        current = current + swapped(current, "leaf", bit_number)
    return current


def local(right_side, diag_inverse, update_factor, live_blocks):
    leaf_count = lax.axis_size("leaf")
    block_count = lax.axis_size("blk")
    levels = leaf_count.bit_length()
    leaf_index = lax.axis_index("leaf")
    block_index = lax.axis_index("blk")
    block_rows = diag_inverse.shape[2]
    vectors = right_side.shape[0]
    level_width = block_count * block_rows
    rows_all = leaf_count * level_width
    flat_side = right_side.reshape(vectors, 1, levels * block_rows)
    every_side = lax.all_gather(flat_side, ("leaf", "blk"), axis=1, tiled=True)
    inverse_rows = diag_inverse.reshape(block_rows, -1)
    update_rows = update_factor.reshape(block_rows, -1)
    orders = [(1 << height) * level_width for height in range(levels)]
    spans = [sum(orders[height + 1 :]) for height in range(levels)]
    update_start = [sum(spans[:height]) for height in range(levels)]
    contract_second = (((1,), (1,)), ((), ()))
    own_masks = []
    group_masks = []
    own_starts = []
    group_starts = []
    inverse_parts = []
    update_parts = []
    for height in range(levels):
        group_index = leaf_index >> height
        local_rank = leaf_index & (1 << height) - 1
        offset = 2 * leaf_count - (2 * leaf_count >> height)
        live_count = live_blocks[offset + group_index]
        own_position = local_rank * block_count + block_index
        own_masks.append((own_position < live_count).astype(jnp.float32))
        block_alive = (jnp.arange((1 << height) * block_count) < live_count).astype(jnp.float32)
        group_masks.append(jnp.repeat(block_alive, block_rows))
        own_starts.append(own_position * block_rows)
        group_starts.append(group_index * orders[height])
        start = ((1 << height) - 1) * level_width
        inverse_parts.append(inverse_rows[:, start : start + orders[height]])
        update_parts.append(
            update_rows[:, update_start[height] : update_start[height] + spans[height]]
        )
    pending = [jnp.zeros((vectors, orders[height]), jnp.float32) for height in range(levels)]
    forward = []
    for height in range(levels):
        level_side = every_side[:, :, height * block_rows : (height + 1) * block_rows].reshape(
            vectors, rows_all
        )
        source = lax.dynamic_slice_in_dim(level_side, group_starts[height], orders[height], 1)
        if height > 0:
            source = source - group_sum(pending[height], height)
        reduced = (group_masks[height] * source).astype(jnp.bfloat16)
        solved = own_masks[height] * lax.dot_general(
            reduced, inverse_parts[height], contract_second, preferred_element_type=jnp.float32
        )
        forward.append(solved)
        if height < levels - 1:
            spread = jnp.dot(
                solved.astype(jnp.bfloat16),
                update_parts[height],
                preferred_element_type=jnp.float32,
            )
            cursor = 0
            for ancestor in range(height + 1, levels):
                pending[ancestor] = (
                    pending[ancestor] + spread[:, cursor : cursor + orders[ancestor]]
                )
                cursor += orders[ancestor]
    whole_solved = [None] * levels
    backward = [None] * levels
    for height in reversed(range(levels)):
        residual = forward[height]
        if height < levels - 1:
            ancestors = jnp.concatenate(
                [whole_solved[ancestor] for ancestor in range(height + 1, levels)], axis=1
            )
            residual = residual - lax.dot_general(
                ancestors, update_parts[height], contract_second, preferred_element_type=jnp.float32
            )
        weighted = (own_masks[height] * residual).astype(jnp.bfloat16)
        partial_value = jnp.dot(weighted, inverse_parts[height], preferred_element_type=jnp.float32)
        supernode_solved = group_masks[height] * group_sum(partial_value, height)
        backward[height] = lax.dynamic_slice_in_dim(
            supernode_solved, own_starts[height], block_rows, 1
        )
        whole_solved[height] = supernode_solved.astype(jnp.bfloat16)
    forward_out = jnp.stack(forward, axis=1).reshape(vectors, 1, 1, levels * block_rows)
    backward_out = jnp.stack(backward, axis=1).reshape(vectors, 1, 1, levels * block_rows)
    return (forward_out, backward_out)


def solution(mesh):
    in_specs = (
        P(None, "leaf", "blk", None),
        P("leaf", "blk", None, None),
        P("leaf", "blk", None, None),
        P(),
    )
    out_specs = (P(None, "leaf", "blk", None), P(None, "leaf", "blk", None))
    return jax.shard_map(local, mesh=mesh, in_specs=in_specs, out_specs=out_specs, check_vma=False)
```

profile of v0, /device:TPU:0, one launch (start us, length us, event | category | flops | bytes accessed | tf_op | source)
XLA Modules:
  0.0 352.7 jit_solution(483365086368205140)
XLA Ops:
  7.2 0.0 copy-start
  7.2 0.0 all-reduce.3.cloned.1.call-start
  7.2 71.2 %all-gather = f32[4,32,1,384]{3,2,1,0:T(1,128)S(1)} all-gather(f32[4,1,1,384]{3,2,1,0:T(1,128)} %param.4), channel_id=2, replica_groups=mesh['leaf'=4,'blk'=8] {'leaf','blk'}, dimensions={1}, use_global_device_ids=true | all-gather | bytes 202752 | tf_op jit(solution)/shard_map/all_gather | solution.py:35
  78.5 1.4 fusion.53
  80.0 0.6 compare_convert_fusion.2
  80.6 0.1 broadcast_bitcast_fusion.2
  81.3 1.1 convolution_multiply_fusion.1
  82.5 1.7 fusion.2
  84.2 33.0 %psum.35 = f32[4,2048]{1,0:T(4,128)S(1)} all-reduce(f32[4,2048]{1,0:T(4,128)S(1)} %slice.44), channel_id=1, replica_groups=mesh['leaf'=4,'blk'=8] {'blk'}, use_global_device_ids=true, to_apply=%region_0.0 | all-reduce | flops 8192 | bytes 65536 | tf_op jit(solution)/shard_map/psum | solution.py:18
  117.2 0.0 collective-permute-start
  117.2 0.6 compare_convert_fusion.1
  117.9 0.1 broadcast_bitcast_fusion.1
  118.6 0.0 collective-permute-done
  118.6 0.0 copy-done
  118.6 0.2 convolution_multiply_fusion.2
  118.9 2.1 convolution_add_fusion
  121.0 0.0 all-reduce.3.cloned.1.call-update
  121.0 0.0 all-reduce.5.cloned.1.call-start
  121.1 65.9 %all-reduce.3.cloned.1.call-done = f32[4,4096]{1,0:T(4,128)} async-done(((f32[4,4096]{1,0:T(4,128)}), f32[4,4096]{1,0:T(4,128)}) %all-reduce.3.cloned.1.call-update) | async-done | bytes 65552 | tf_op jit(solution)/shard_map/psum | solution.py:18
  186.9 0.0 collective-permute-start.1
  186.9 0.6 compare_convert_fusion
  187.6 0.8 collective-permute-done.1
  188.4 0.9 add.75
  189.3 1.5 collective-permute-start.2
  190.8 0.1 broadcast_bitcast_fusion
  191.5 2.1 collective-permute-done.2
  193.6 0.4 convolution_multiply_fusion
  194.0 0.9 fusion.19
  194.9 0.0 all-reduce.5.cloned.1.call-update
  194.9 69.3 %all-reduce.5.cloned.1.call-done = f32[4,4096]{1,0:T(4,128)} async-done(((f32[4,4096]{1,0:T(4,128)}), f32[4,4096]{1,0:T(4,128)}) %all-reduce.5.cloned.1.call-update) | async-done | bytes 65552 | tf_op jit(solution)/shard_map/psum | solution.py:18
  264.2 0.0 collective-permute-start.3
  264.2 0.1 dynamic-slice
  264.3 1.4 collective-permute-done.3
  265.7 0.9 add.77
  266.5 1.5 collective-permute-start.4
  268.1 0.6 copy.6
  268.7 2.2 collective-permute-done.4
  270.9 1.9 fusion.18
  272.8 36.1 %psum.38 = f32[4,2048]{1,0:T(4,128)S(1)} all-reduce(f32[4,2048]{1,0:T(4,128)S(1)} %fusion.18), channel_id=1, replica_groups=mesh['leaf'=4,'blk'=8] {'blk'}, use_global_device_ids=true, to_apply=%region_3.0 | all-reduce | flops 8192 | bytes 65536 | tf_op jit(solution)/shard_map/psum | solution.py:18
  308.9 0.0 collective-permute-start.5
  308.9 1.2 collective-permute-done.5
  310.2 2.1 fusion.16
  312.3 33.0 %psum.39 = f32[4,1024]{1,0:T(4,128)S(1)} all-reduce(f32[4,1024]{1,0:T(4,128)S(1)} %fusion.16), channel_id=1, replica_groups=mesh['leaf'=4,'blk'=8] {'blk'}, use_global_device_ids=true, to_apply=%region_4.0 | all-reduce | flops 4096 | bytes 32768 | tf_op jit(solution)/shard_map/psum | solution.py:18
  345.3 0.6 copy.7
  (12 shorter events, 0.2 us)
Async XLA Ops:
  7.2 111.5 %copy-start = (bf16[1,1,128,7168]{3,2,1,0:T(8,128)(2,1)S(1)}, bf16[1,1,128,7168]{3,2,1,0:T(8,128)(2,1)}, u32[]{:S(2)}) copy-start(bf16[1,1,128,7168]{3,2,1,0:T(8,128)(2,1)} %param.5) | copy-start | bytes 5505028
  7.2 179.8 %all-reduce.3.cloned.1.call-start = ((), (), s32[]{:S(2)}) async-start(), calls=%async_computation | async-start | bytes 131072 | tf_op jit(solution)/shard_map/psum | solution.py:18
  117.2 1.4 collective-permute-start
  121.0 143.2 %all-reduce.5.cloned.1.call-start = ((), (), s32[]{:S(2)}) async-start(), calls=%async_computation.1 | async-start | bytes 131072 | tf_op jit(solution)/shard_map/psum | solution.py:18
  186.9 1.5 collective-permute-start.1
  189.3 4.3 %collective-permute-start.2 = (f32[4,4096]{1,0:T(4,128)S(1)}, f32[4,4096]{1,0:T(4,128)S(1)}, u32[]{:S(2)}, u32[]{:S(2)}) collective-permute-start(f32[4,4096]{1,0:T(4,128)S(1)} %add.75), channel_id=1, source_target_pairs={{0,16},{16,0},{8,24},{24,8},{1,17},{17,1},{9,25},{25,9},{2,18},{18... | collective-permute-start | bytes 196616 | tf_op jit(solution)/shard_map/ppermute | solution.py:14
  264.2 1.5 collective-permute-start.3
  266.5 4.3 %collective-permute-start.4 = (f32[4,4096]{1,0:T(4,128)S(1)}, f32[4,4096]{1,0:T(4,128)S(1)}, u32[]{:S(2)}, u32[]{:S(2)}) collective-permute-start(f32[4,4096]{1,0:T(4,128)S(1)} %add.77), channel_id=1, source_target_pairs={{0,16},{16,0},{8,24},{24,8},{1,17},{17,1},{9,25},{25,9},{2,18},{18... | collective-permute-start | bytes 196616 | tf_op jit(solution)/shard_map/ppermute | solution.py:14
  308.9 1.2 collective-permute-start.5
Sparse Core Ops, SparseCore 0:
  121.2 65.7 all-reduce.2
  195.0 69.1 all-reduce.4
where the time goes:
time: 353 us
  blocking collectives  173 us (49%)
  waiting for transfers between devices  143 us (41%)
  between operations  16.1 us (5%)
  matrix products  10.5 us (3%)
  other arithmetic  3.71 us (1%)
    psum x2, waiting for transfers between devices, group_sum(): current = lax.psum(partial_value, 'blk')  135 us
    psum x3, blocking collectives, group_sum(): current = lax.psum(partial_value, 'blk')  102 us
    all_gather x1, blocking collectives, local(): every_side = lax.all_gather(flat_side, ('leaf', 'blk'), axis=1, tiled=True)  71.2 us
    ppermute x6, waiting for transfers between devices, swapped(): return lax.ppermute(block, axis, route)  7.66 us
  transfers between devices with their start and end apart: 8, of which 7 were waited for; matrix products, arithmetic and copies ran while one was open for 1% of the time, Pallas kernels for 0%

commit v1 on v0

--- a/solution.py
+++ b/solution.py
@@ -15,7 +15,7 @@
 
 
 def group_sum(partial_value, height):
-    current = lax.psum(partial_value, "blk")
+    current = jnp.sum(lax.all_gather(partial_value, "blk"), axis=0)
     for bit_number in range(height):
         current = current + swapped(current, "leaf", bit_number)
     return current

time: 353 us -> 254 us (0.72)
  waiting for transfers between devices: 143 us -> 8.9 us
  blocking collectives: 173 us -> 226 us
  between operations: 16.1 us -> 2.81 us
    all_gather x0 -> x5, blocking collectives: none -> 155 us  [group_sum(): current = jnp.sum(lax.all_gather(partial_value, 'blk'), axis=0)]
    psum x2 -> x0, waiting for transfers between devices: 135 us -> none  [group_sum(): current = lax.psum(partial_value, 'blk')]
    psum x3 -> x0, blocking collectives: 102 us -> none  [group_sum(): current = lax.psum(partial_value, 'blk')]
  transfers between devices with their start and end apart: 8 -> 6, of which waited for: 7 -> 5; matrix products, arithmetic and copies ran while one was open for 1% -> 1% of each run, Pallas kernels for 0% -> 0%
where the time goes in v1:
time: 254 us
  blocking collectives  226 us (89%)
  matrix products  9.25 us (4%)
  waiting for transfers between devices  8.9 us (4%)
  local copies, waits for them, and re-layouts  3.11 us (1%)
  between operations  2.81 us (1%)
    all_gather x5, blocking collectives, group_sum(): current = jnp.sum(lax.all_gather(partial_value, 'blk'), axis=0)  155 us
    all_gather x1, blocking collectives, local(): every_side = lax.all_gather(flat_side, ('leaf', 'blk'), axis=1, tiled=True)  71.1 us
    ppermute x6, waiting for transfers between devices, swapped(): return lax.ppermute(block, axis, route)  8.9 us
  transfers between devices with their start and end apart: 6, of which 5 were waited for; matrix products, arithmetic and copies ran while one was open for 1% of the time, Pallas kernels for 0%

profile of v1, /device:TPU:0, one launch (start us, length us, event | category | flops | bytes accessed | tf_op | source)
XLA Modules:
  0.0 253.9 jit_solution(12785789002883394261)
XLA Ops:
  0.6 71.1 %all-gather = f32[4,32,1,384]{3,2,1,0:T(1,128)S(1)} all-gather(f32[4,1,1,384]{3,2,1,0:T(1,128)} %param.4), channel_id=2, replica_groups=mesh['leaf'=4,'blk'=8] {'leaf','blk'}, dimensions={1}, use_global_device_ids=true | all-gather | bytes 202752 | tf_op jit(solution)/shard_map/all_gather | solution.py:35
  71.7 0.0 copy-start
  71.8 1.5 fusion.51
  73.3 0.6 compare_convert_fusion.2
  73.9 0.1 broadcast_bitcast_fusion.2
  74.7 1.1 convolution_multiply_fusion.1
  75.8 1.7 fusion.3
  77.5 30.7 %all-gather.6 = f32[8,4,2048]{2,1,0:T(4,128)S(1)} all-gather(f32[1,4,2048]{2,1,0:T(4,128)S(1)} %slice_bitcast_fusion.3), channel_id=3, replica_groups=mesh['leaf'=4,'blk'=8] {'blk'}, dimensions={0}, use_global_device_ids=true | all-gather | bytes 294912 | tf_op jit(solution)/shard_map/all_gather | solution.py:18
  108.3 0.1 collective-permute-start
  108.4 0.7 compare_convert_fusion.1
  109.1 0.1 broadcast_bitcast_fusion.1
  109.9 0.0 collective-permute-done
  109.9 0.0 copy-done
  109.9 0.2 convolution_multiply_fusion.2
  110.2 1.5 fusion
  111.7 31.3 %all-gather.7 = f32[8,4,4096]{2,1,0:T(4,128)S(1)} all-gather(f32[1,4,4096]{2,1,0:T(4,128)S(1)} %fusion), channel_id=4, replica_groups=mesh['leaf'=4,'blk'=8] {'blk'}, dimensions={0}, use_global_device_ids=true | all-gather | bytes 589824 | tf_op jit(solution)/shard_map/all_gather | solution.py:18
  142.9 0.1 reduce_sum.46
  143.0 0.1 collective-permute-start.1
  143.1 0.7 compare_convert_fusion
  143.8 0.6 collective-permute-done.1
  144.4 0.7 collective-permute-start.2
  145.1 0.1 broadcast_bitcast_fusion
  145.8 2.9 %collective-permute-done.2 = f32[4,4096]{1,0:T(4,128)S(1)} collective-permute-done((f32[4,4096]{1,0:T(4,128)S(1)}, f32[4,4096]{1,0:T(4,128)S(1)}, u32[]{:S(2)}, u32[]{:S(2)}) %collective-permute-start.2) | collective-permute-done | bytes 65568 | tf_op jit(solution)/shard_map/ppermute | solution.py:14
  148.7 0.4 convolution_multiply_fusion
  149.1 0.3 convolution_bitcast_fusion
  149.3 31.3 %all-gather.8 = f32[8,4,4096]{2,1,0:T(4,128)S(1)} all-gather(f32[1,4,4096]{2,1,0:T(4,128)S(1)} %convolution_bitcast_fusion), channel_id=5, replica_groups=mesh['leaf'=4,'blk'=8] {'blk'}, dimensions={0}, use_global_device_ids=true | all-gather | bytes 589824 | tf_op jit(solution)/shard_map/all_gather | solution.py:18
  180.7 0.1 reduce_sum.47
  180.7 0.1 collective-permute-start.3
  180.8 0.1 dynamic-slice
  180.9 1.2 collective-permute-done.3
  182.1 0.7 collective-permute-start.4
  182.8 0.6 copy.8
  183.4 3.0 %collective-permute-done.4 = f32[4,4096]{1,0:T(4,128)S(1)} collective-permute-done((f32[4,4096]{1,0:T(4,128)S(1)}, f32[4,4096]{1,0:T(4,128)S(1)}, u32[]{:S(2)}, u32[]{:S(2)}) %collective-permute-start.4) | collective-permute-done | bytes 65568 | tf_op jit(solution)/shard_map/ppermute | solution.py:14
  186.5 1.9 convolution_bitcast_fusion.1
  188.4 30.8 %all-gather.9 = f32[8,4,2048]{2,1,0:T(4,128)S(1)} all-gather(f32[1,4,2048]{2,1,0:T(4,128)S(1)} %convolution_bitcast_fusion.1), channel_id=6, replica_groups=mesh['leaf'=4,'blk'=8] {'blk'}, dimensions={0}, use_global_device_ids=true | all-gather | bytes 294912 | tf_op jit(solution)/shard_map/all_gather | solution.py:18
  219.2 0.1 collective-permute-start.5
  219.3 1.2 collective-permute-done.5
  220.5 2.1 convolution_bitcast_fusion.2
  222.6 30.6 %all-gather.10 = f32[8,4,1024]{2,1,0:T(4,128)S(1)} all-gather(f32[1,4,1024]{2,1,0:T(4,128)S(1)} %convolution_bitcast_fusion.2), channel_id=7, replica_groups=mesh['leaf'=4,'blk'=8] {'blk'}, dimensions={0}, use_global_device_ids=true | all-gather | bytes 147456 | tf_op jit(solution)/shard_map/all_gather | solution.py:18
  253.3 0.6 copy.9
  (17 shorter events, 0.4 us)
Async XLA Ops:
  71.7 38.2 %copy-start = (bf16[1,1,128,7168]{3,2,1,0:T(8,128)(2,1)S(1)}, bf16[1,1,128,7168]{3,2,1,0:T(8,128)(2,1)}, u32[]{:S(2)}) copy-start(bf16[1,1,128,7168]{3,2,1,0:T(8,128)(2,1)} %param.5) | copy-start | bytes 5505028
  108.3 1.6 collective-permute-start
  143.0 1.3 collective-permute-start.1
  144.4 4.3 %collective-permute-start.2 = (f32[4,4096]{1,0:T(4,128)S(1)}, f32[4,4096]{1,0:T(4,128)S(1)}, u32[]{:S(2)}, u32[]{:S(2)}) collective-permute-start(f32[4,4096]{1,0:T(4,128)S(1)} %add.65), channel_id=1, source_target_pairs={{0,16},{16,0},{8,24},{24,8},{1,17},{17,1},{9,25},{25,9},{2,18},{18... | collective-permute-start | bytes 196616 | tf_op jit(solution)/shard_map/ppermute | solution.py:14
  180.7 1.3 collective-permute-start.3
  182.1 4.3 %collective-permute-start.4 = (f32[4,4096]{1,0:T(4,128)S(1)}, f32[4,4096]{1,0:T(4,128)S(1)}, u32[]{:S(2)}, u32[]{:S(2)}) collective-permute-start(f32[4,4096]{1,0:T(4,128)S(1)} %add.67), channel_id=1, source_target_pairs={{0,16},{16,0},{8,24},{24,8},{1,17},{17,1},{9,25},{25,9},{2,18},{18... | collective-permute-start | bytes 196616 | tf_op jit(solution)/shard_map/ppermute | solution.py:14
  219.2 1.3 collective-permute-start.5
